TPU v7x, 32 devices: a whole 2x2x4 slice. The times are simulated.
32 devices in a mesh: groups: 2 (over y), slab: 4 (over z), pencil: 2 (over x), comp: 2 (over core).
Axes of the slice: x: 2, y: 2, z: 4, core: 2. Of those that a mesh axis runs over, the one named last changes fastest.
Arguments:
- u_start: float32 [3, 64, 64, 512], P(None, ('groups', 'slab'), 'pencil', 'comp'), parts along dimension 1, may hold values from -6 to 6
- toughness: float32 [64, 64, 512], P(('groups', 'slab'), 'pencil', 'comp'), parts along dimension 0, may hold values from 0.3 to 1.5
- crack_label: int32 [64, 64, 512], P(('groups', 'slab'), 'pencil', 'comp'), parts along dimension 0, may hold values from 0 to 2
- obs_weight: bfloat16 [32, 64, 2, 4096], P('slab', 'pencil', 'comp'), may hold values from -0.75 to 0.75
- sensor_cell: int32 [4096], replicated, may hold values from 0 to 4095
Outputs:
- moved: float32 [3, 64, 64, 512], P(None, ('groups', 'slab'), 'pencil', 'comp'), parts along dimension 1
- damage: float32 [64, 64, 512], P(('groups', 'slab'), 'pencil', 'comp'), parts along dimension 0
- readings: float32 [3, 8192], P(None, 'groups'), parts along dimension 1
There are 2 independent parts, one for each index of `groups`. A program takes and returns all parts, laid end to end along the dimension named above; an argument that names none is the same for every part. Nothing has to cross between parts.
Inputs may be any that keep to these rules, and one draw needn't show every extreme that they name: `sensor_cell`: numbers cell blocks as (64 z + y) * 2 + h. `crack_label`: 0 intact, 1 partly cracked, 2 cracked.
All inputs are finite; a program needn't handle non-finite values.
Results may differ from a plain program's by a relative error of at most 0.003.
Values sent between devices are 32-bit elements; how exact they have to be, the bound alone decides.
A program may use at most 128 MiB of HBM per device.

v0:
```python
import jax
import jax.numpy as jnp
from jax import lax
from jax.sharding import PartitionSpec as P

SHEAR_MODULUS = 1.0
LAME_FIRST = 1.5
RESIDUAL_STIFF = 0.001
TIME_DISP = 0.15
TIME_DAMAGE = 0.08
LENGTH_SCALE = 1.0
DAMAGE_LEVEL = 0.45
POINT_GAIN = 8.0


def with_halo(block, sides, width):
    for axis, dim in sides:
        count = lax.axis_size(axis)
        forward = [(i, i + 1) for i in range(count - 1)]
        backward = [(target, source) for source, target in forward]
        low = lax.ppermute(
            lax.slice_in_dim(block, block.shape[dim] - width, None, axis=dim), axis, forward
        )
        high = lax.ppermute(lax.slice_in_dim(block, 0, width, axis=dim), axis, backward)
        block = jnp.concatenate([low, block, high], axis=dim)
    return block


def central(source, spatial):
    if spatial == 0:
        return 0.5 * (source[..., 2:, 1:-1, 1:-1] - source[..., :-2, 1:-1, 1:-1])
    if spatial == 1:
        return 0.5 * (source[..., 1:-1, 2:, 1:-1] - source[..., 1:-1, :-2, 1:-1])
    return 0.5 * (source[..., 1:-1, 1:-1, 2:] - source[..., 1:-1, 1:-1, :-2])


def shrink(source):
    return source[..., 1:-1, 1:-1, 1:-1]


def laplace(source):
    return (
        source[2:, 1:-1, 1:-1]
        + source[:-2, 1:-1, 1:-1]
        + source[1:-1, 2:, 1:-1]
        + source[1:-1, :-2, 1:-1]
        + source[1:-1, 1:-1, 2:]
        + source[1:-1, 1:-1, :-2]
        - 6.0 * source[1:-1, 1:-1, 1:-1]
    )


def entry_key(first, second):
    return (min(first, second), max(first, second))


def rotate(matrix, first, second):
    other = 3 - first - second
    diag_first = matrix[first, first]
    diag_second = matrix[second, second]
    coupling = matrix[first, second]
    angle = 0.5 * jnp.arctan2(2.0 * coupling, diag_second - diag_first)
    cosine = jnp.cos(angle)
    sine = jnp.sin(angle)
    side_first = matrix[entry_key(other, first)]
    side_second = matrix[entry_key(other, second)]
    result = dict(matrix)
    result[first, first] = (
        cosine * cosine * diag_first - 2.0 * cosine * sine * coupling + sine * sine * diag_second
    )
    result[second, second] = (
        sine * sine * diag_first + 2.0 * cosine * sine * coupling + cosine * cosine * diag_second
    )
    result[first, second] = jnp.zeros_like(coupling)
    result[entry_key(other, first)] = cosine * side_first - sine * side_second
    result[entry_key(other, second)] = sine * side_first + cosine * side_second
    return result


def eigenvalues(matrix):
    for sweep_index in range(5):
        for first, second in ((0, 1), (0, 2), (1, 2)):
            matrix = rotate(matrix, first, second)
    return [matrix[0, 0], matrix[1, 1], matrix[2, 2]]


def advance(padded_disp, padded_damage, toughness):
    gradient = [
        [central(padded_disp[component], direction) for direction in range(3)]
        for component in range(3)
    ]
    strain = {}
    for first in range(3):
        for second in range(first, 3):
            strain[first, second] = 0.5 * (gradient[first][second] + gradient[second][first])
    trace_full = strain[0, 0] + strain[1, 1] + strain[2, 2]
    damage_mid = shrink(padded_damage)
    degrade = (1.0 - damage_mid) ** 2 + RESIDUAL_STIFF
    divergence = []
    for component in range(3):
        total_force = 0.0
        for direction in range(3):
            stress = 2.0 * SHEAR_MODULUS * strain[entry_key(component, direction)]
            if component == direction:
                stress = stress + LAME_FIRST * trace_full
            total_force = total_force + central(degrade * stress, direction)
        divergence.append(total_force)
    moved = shrink(shrink(padded_disp)) + TIME_DISP * jnp.stack(divergence)
    inner = {key_pair: shrink(entry_value) for key_pair, entry_value in strain.items()}
    trace_inner = shrink(trace_full)
    energy = 0.5 * LAME_FIRST * jnp.maximum(trace_inner, 0.0) ** 2
    for eigen_value in eigenvalues(inner):
        energy = energy + SHEAR_MODULUS * jnp.maximum(eigen_value, 0.0) ** 2
    damage_core = shrink(damage_mid)
    damage = damage_core + TIME_DAMAGE * (
        2.0 * (1.0 - damage_core) * energy
        - toughness / LENGTH_SCALE * damage_core
        + toughness * LENGTH_SCALE * laplace(damage_mid)
    )
    return (moved, damage)


def local(u_start, toughness, crack_label, obs_weight, sensor_cell):
    planes, rows, columns = toughness.shape
    damage = DAMAGE_LEVEL * crack_label.astype(jnp.float32)
    moved = u_start
    for repeat in range(2):
        stacked = jnp.concatenate([moved, damage[None]], axis=0)
        padded = with_halo(stacked, (("slab", 1), ("pencil", 2), ("comp", 3)), 2)
        moved, damage = advance(padded[:3], padded[3], toughness)
    pooled = jnp.mean(moved, axis=-1).reshape(3, planes * rows).astype(jnp.bfloat16)
    weight_rows = obs_weight.reshape(planes * rows, obs_weight.shape[-1])
    dense = jnp.dot(pooled, weight_rows, preferred_element_type=jnp.float32)
    plane_ids = lax.axis_index("slab") * planes + jnp.arange(planes, dtype=jnp.int32)
    row_ids = lax.axis_index("pencil") * rows + jnp.arange(rows, dtype=jnp.int32)
    block_ids = (
        (plane_ids[:, None] * (rows * lax.axis_size("pencil")) + row_ids[None, :])
        * lax.axis_size("comp")
        + lax.axis_index("comp")
    ).reshape(planes * rows)
    picks = (block_ids[:, None] == sensor_cell[None, :]).astype(jnp.bfloat16)
    point = jnp.dot(pooled, picks, preferred_element_type=jnp.float32)
    partial_sum = dense + POINT_GAIN * point
    readings = lax.psum(partial_sum, ("slab", "pencil", "comp"))
    return (moved, damage, readings)


def solution(mesh):
    return jax.shard_map(
        local,
        mesh=mesh,
        in_specs=(
            P(None, ("groups", "slab"), "pencil", "comp"),
            P(("groups", "slab"), "pencil", "comp"),
            P(("groups", "slab"), "pencil", "comp"),
            P("slab", "pencil", "comp", None),
            P(),
        ),
        out_specs=(
            P(None, ("groups", "slab"), "pencil", "comp"),
            P(("groups", "slab"), "pencil", "comp"),
            P(None, "groups"),
        ),
        check_vma=False,
    )
```

profile of v0, /device:TPU:0, one launch (start us, length us, event | category | flops | bytes accessed | tf_op | source)
XLA Modules:
  0.0 226.6 jit_solution(18250146474018214217)
XLA Ops:
  2.9 5.0 %collective-permute-start = (f32[4,2,32,256]{3,2,1,0:T(8,128)S(1)}, f32[4,2,32,256]{3,2,1,0:T(8,128)S(1)}, u32[]{:S(2)}, u32[]{:S(2)}) collective-permute-start(f32[4,2,32,256]{3,2,1,0:T(8,128)S(1)} %get-tuple-element.66), channel_id=1, source_target_pairs={{0,4},{4,8},{8,12},{1,5},{5,9},{9,13},{2,6},{6,10},{10,14},{3,7},{... | collective-permute-start | bytes 786440 | tf_op jit(solution)/shard_map/ppermute | solution.py:21
  9.1 4.2 %collective-permute-done = f32[4,2,32,256]{3,2,1,0:T(8,128)S(1)} collective-permute-done((f32[4,2,32,256]{3,2,1,0:T(8,128)S(1)}, f32[4,2,32,256]{3,2,1,0:T(8,128)S(1)}, u32[]{:S(2)}, u32[]{:S(2)}) %collective-permute-start) | collective-permute-done | bytes 262176 | tf_op jit(solution)/shard_map/ppermute | solution.py:21
  13.4 4.1 %collective-permute-done.1 = f32[4,2,32,256]{3,2,1,0:T(8,128)S(1)} collective-permute-done((f32[4,2,32,256]{3,2,1,0:T(8,128)S(1)}, f32[4,2,32,256]{3,2,1,0:T(8,128)S(1)}, u32[]{:S(2)}, u32[]{:S(2)}) %collective-permute-start.1) | collective-permute-done | bytes 262176 | tf_op jit(solution)/shard_map/ppermute | solution.py:24
  18.7 3.4 %collective-permute-start.2 = (f32[4,12,2,256]{3,2,1,0:T(2,128)S(1)}, f32[4,12,2,256]{3,2,1,0:T(2,128)S(1)}, u32[]{:S(2)}, u32[]{:S(2)}) collective-permute-start(f32[4,12,2,256]{3,2,1,0:T(2,128)S(1)} %get-tuple-element.58), channel_id=1, source_target_pairs={{0,2},{1,3},{4,6},{5,7},{8,10},{9,11},{12,14},{13,15},{16,18},{17,... | collective-permute-start | bytes 294920 | tf_op jit(solution)/shard_map/ppermute | solution.py:21
  24.3 4.3 %collective-permute-done.3 = f32[4,12,2,256]{3,2,1,0:T(2,128)S(1)} collective-permute-done((f32[4,12,2,256]{3,2,1,0:T(2,128)S(1)}, f32[4,12,2,256]{3,2,1,0:T(2,128)S(1)}, u32[]{:S(2)}, u32[]{:S(2)}) %collective-permute-start.3) | collective-permute-done | bytes 98336 | tf_op jit(solution)/shard_map/ppermute | solution.py:24
  28.9 1.6 fusion.80
  30.5 1.6 copy.24
  32.2 1.9 collective-permute-start.4
  34.1 2.2 copy.25
  37.6 2.2 copy.26
  39.8 2.2 copy.27
  42.0 3.1 %pad_maximum_fusion = f32[4,12,36,260]{3,2,1,0:T(8,128)S(1)} fusion(f32[4,12,36,2]{3,2,1,0:T(8,128)} %copy.27, f32[4,12,2,256]{3,2,1,0:T(2,128)} %copy-done.13, f32[4,2,32,256]{3,2,1,0:T(8,128)} %copy-done.5, f32[1,8,32,256]{3,2,1,0:T(8,128)S(1)} %multiply_bitcast_fusion, f32[3,8,32,256]{3,2,1,0:T(8,128)S(1)} %copy-done.1, ...), kind=kLoop, calls=%fused_computation.3 | loop fusion | flops 3144960 | bytes 3594240 | tf_op jit(solution)/shard_map/concatenate | solution.py:25
  45.3 2.2 multiply_multiply_fusion.5
  50.1 29.3 %fusion.51 = f32[1,8,32,256]{3,2,1,0:T(8,128)S(1)} fusion(f32[8,32,256]{2,1,0:T(8,128)S(1)} %copy-done.15, f32[12,36,260]{2,1,0:T(8,128)S(1)} %get-tuple-element.37, f32[10,34,258]{2,1,0:T(8,128)S(1)} %get-tuple-element.46, f32[10,34,258]{2,1,0:T(8,128)S(1)} %get-tuple-element.47, f32[10,34,258]{2,1,0:T(8,128)S(1)} %get-tuple-element.29, ...), kind=kLoop, calls=%fused_computation.127 | loop fusion | flops 23068672 | bytes 4194304 | tf_op jit(solution)/shard_map/broadcast_in_dim | solution.py:128
  80.3 3.5 %collective-permute-start.6 = (f32[4,2,32,256]{3,2,1,0:T(8,128)}, f32[4,2,32,256]{3,2,1,0:T(8,128)S(1)}, u32[]{:S(2)}, u32[]{:S(2)}) collective-permute-start(f32[4,2,32,256]{3,2,1,0:T(8,128)} %get-tuple-element.64), channel_id=1, source_target_pairs={{0,4},{4,8},{8,12},{1,5},{5,9},{9,13},{2,6},{6,10},{10,14},{3,7},{... | collective-permute-start | bytes 786440 | tf_op jit(solution)/shard_map/ppermute | solution.py:21
  85.7 4.3 %collective-permute-done.6 = f32[4,2,32,256]{3,2,1,0:T(8,128)S(1)} collective-permute-done((f32[4,2,32,256]{3,2,1,0:T(8,128)}, f32[4,2,32,256]{3,2,1,0:T(8,128)S(1)}, u32[]{:S(2)}, u32[]{:S(2)}) %collective-permute-start.6) | collective-permute-done | bytes 262176 | tf_op jit(solution)/shard_map/ppermute | solution.py:21
  90.0 4.7 %collective-permute-done.7 = f32[4,2,32,256]{3,2,1,0:T(8,128)} collective-permute-done((f32[4,2,32,256]{3,2,1,0:T(8,128)}, f32[4,2,32,256]{3,2,1,0:T(8,128)}, u32[]{:S(2)}, u32[]{:S(2)}) %collective-permute-start.7) | collective-permute-done | bytes 262176 | tf_op jit(solution)/shard_map/ppermute | solution.py:24
  95.9 1.5 collective-permute-start.8
  100.0 4.1 %collective-permute-done.9 = f32[4,12,2,256]{3,2,1,0:T(2,128)S(1)} collective-permute-done((f32[4,12,2,256]{3,2,1,0:T(2,128)S(1)}, f32[4,12,2,256]{3,2,1,0:T(2,128)S(1)}, u32[]{:S(2)}, u32[]{:S(2)}) %collective-permute-start.9) | collective-permute-done | bytes 98336 | tf_op jit(solution)/shard_map/ppermute | solution.py:24
  104.1 1.5 pad_maximum_fusion.3
  105.6 1.6 fusion.79
  107.2 1.6 copy.28
  108.8 1.9 collective-permute-start.10
  110.7 2.2 copy.29
  117.0 2.2 copy.30
  119.2 2.2 copy.31
  121.4 3.3 %pad_maximum_fusion.1 = f32[4,12,36,260]{3,2,1,0:T(8,128)S(1)} fusion(f32[4,12,36,2]{3,2,1,0:T(8,128)} %copy.31, f32[4,12,2,256]{3,2,1,0:T(2,128)} %copy-done.12, f32[4,2,32,256]{3,2,1,0:T(8,128)} %collective-permute-done.7, f32[1,8,32,256]{3,2,1,0:T(8,128)S(1)} %fusion.51, f32[3,8,32,256]{3,2,1,0:T(8,128)} %copy-done.2, ...), kind=kLoop, calls=%fused_computation.4 | loop fusion | flops 3144960 | bytes 3594240 | tf_op jit(solution)/shard_map/concatenate | solution.py:25
  124.9 3.8 %multiply_multiply_fusion.2 = (f32[10,34,258]{2,1,0:T(8,128)S(1)}, f32[10,34,258]{2,1,0:T(8,128)}, f32[10,34,258]{2,1,0:T(8,128)S(1)}, f32[10,34,258]{2,1,0:T(8,...) fusion(f32[12,36,260]{2,1,0:T(8,128)S(1)} %get-tuple-element.33, ...), kind=kLoop, calls=%fused_computation.61 | loop fusion | flops 2456160 | bytes 8421120 | tf_op jit(solution)/shard_map/mul | solution.py:106
  128.7 2.1 multiply_multiply_fusion
  133.6 1.4 fusion
  135.0 60.5 %psum.7 = f32[3,4096]{1,0:T(4,128)} all-reduce(f32[3,4096]{1,0:T(4,128)} %fusion), channel_id=1, replica_groups=mesh['groups'=2,'slab'=4,'pencil'=2,'comp'=2] {'slab','pencil','comp'}, use_global_device_ids=true, to_apply=%region_1.0 | all-reduce | flops 12288 | bytes 98304 | tf_op jit(solution)/shard_map/psum | solution.py:144
  195.5 31.0 %fusion.26 = f32[8,32,256]{2,1,0:T(8,128)} fusion(f32[8,32,256]{2,1,0:T(8,128)} %param.6, f32[12,36,260]{2,1,0:T(8,128)S(1)} %copy-done.4, f32[10,34,258]{2,1,0:T(8,128)S(1)} %get-tuple-element.39, f32[10,34,258]{2,1,0:T(8,128)} %get-tuple-element.40, f32[10,34,258]{2,1,0:T(8,128)} %get-tuple-element.18, f32[10,34,258]{2,1,0:T(8,128)} %get-tuple-element.44, ...), kind=kLoop, calls=%fused_computation.82 | loop fusion | flops 23068672 | bytes 4194304 | tf_op jit(solution)/shard_map/add | solution.py:115
  (66 shorter events, 24.4 us)
Async XLA Ops:
  0.6 132.5 %copy-start = (bf16[8,32,1,4096]{3,1,2,0:T(8,128)(2,1)S(1)}, bf16[8,32,1,4096]{3,1,2,0:T(8,128)(2,1)}, u32[]{:S(2)}) copy-start(bf16[8,32,1,4096]{3,1,2,0:T(8,128)(2,1)} %param.8) | copy-start | bytes 6291460
  0.6 28.0 %copy-start.1 = (f32[3,8,32,256]{3,2,1,0:T(8,128)S(1)}, f32[3,8,32,256]{3,2,1,0:T(8,128)}, u32[]{:S(2)}) copy-start(f32[3,8,32,256]{3,2,1,0:T(8,128)} %param.5) | copy-start | bytes 2359300
  2.9 10.5 %collective-permute-start = (f32[4,2,32,256]{3,2,1,0:T(8,128)S(1)}, f32[4,2,32,256]{3,2,1,0:T(8,128)S(1)}, u32[]{:S(2)}, u32[]{:S(2)}) collective-permute-start(f32[4,2,32,256]{3,2,1,0:T(8,128)S(1)} %get-tuple-element.66), channel_id=1, source_target_pairs={{0,4},{4,8},{8,12},{1,5},{5,9},{9,13},{2,6},{6,10},{10,14},{3,7},{... | collective-permute-start | bytes 786440 | tf_op jit(solution)/shard_map/ppermute | solution.py:21
  7.8 9.7 %collective-permute-start.1 = (f32[4,2,32,256]{3,2,1,0:T(8,128)S(1)}, f32[4,2,32,256]{3,2,1,0:T(8,128)S(1)}, u32[]{:S(2)}, u32[]{:S(2)}) collective-permute-start(f32[4,2,32,256]{3,2,1,0:T(8,128)S(1)} %get-tuple-element.67), channel_id=1, source_target_pairs={{4,0},{8,4},{12,8},{5,1},{9,5},{13,9},{6,2},{10,6},{14,10},{7,3},{... | collective-permute-start | bytes 786440 | tf_op jit(solution)/shard_map/ppermute | solution.py:24
  17.5 13.0 %copy-start.5 = (f32[4,2,32,256]{3,2,1,0:T(8,128)}, f32[4,2,32,256]{3,2,1,0:T(8,128)S(1)}, u32[]{:S(2)}) copy-start(f32[4,2,32,256]{3,2,1,0:T(8,128)S(1)} %collective-permute-done.1) | copy-start | bytes 786436
  18.7 5.6 %collective-permute-start.2 = (f32[4,12,2,256]{3,2,1,0:T(2,128)S(1)}, f32[4,12,2,256]{3,2,1,0:T(2,128)S(1)}, u32[]{:S(2)}, u32[]{:S(2)}) collective-permute-start(f32[4,12,2,256]{3,2,1,0:T(2,128)S(1)} %get-tuple-element.58), channel_id=1, source_target_pairs={{0,2},{1,3},{4,6},{5,7},{8,10},{9,11},{12,14},{13,15},{16,18},{17,... | collective-permute-start | bytes 294920 | tf_op jit(solution)/shard_map/ppermute | solution.py:21
  22.1 6.5 %collective-permute-start.3 = (f32[4,12,2,256]{3,2,1,0:T(2,128)S(1)}, f32[4,12,2,256]{3,2,1,0:T(2,128)S(1)}, u32[]{:S(2)}, u32[]{:S(2)}) collective-permute-start(f32[4,12,2,256]{3,2,1,0:T(2,128)S(1)} %get-tuple-element.59), channel_id=1, source_target_pairs={{2,0},{3,1},{6,4},{7,5},{10,8},{11,9},{14,12},{15,13},{18,16},{19,... | collective-permute-start | bytes 294920 | tf_op jit(solution)/shard_map/ppermute | solution.py:24
  28.6 1.9 copy-start.13
  32.2 5.4 %collective-permute-start.4 = (f32[4,12,36,2]{2,0,3,1:T(4,128)S(1)}, f32[4,12,36,2]{2,0,3,1:T(4,128)}, u32[]{:S(2)}, u32[]{:S(2)}) collective-permute-start(f32[4,12,36,2]{2,0,3,1:T(4,128)S(1)} %copy.24), channel_id=1, source_target_pairs={{0,1},{2,3},{4,5},{6,7},{8,9},{10,11},{12,13},{14,15},{16,17},{18,... | collective-permute-start | bytes 41480 | tf_op jit(solution)/shard_map/ppermute | solution.py:21
  36.3 3.5 %collective-permute-start.5 = (f32[4,12,36,2]{2,0,3,1:T(4,128)}, f32[4,12,36,2]{2,0,3,1:T(4,128)}, u32[]{:S(2)}, u32[]{:S(2)}) collective-permute-start(f32[4,12,36,2]{2,0,3,1:T(4,128)} %copy.25), channel_id=1, source_target_pairs={{1,0},{3,2},{5,4},{7,6},{9,8},{11,10},{13,12},{15,14},{17,16},{19,... | collective-permute-start | bytes 41480 | tf_op jit(solution)/shard_map/ppermute | solution.py:24
  48.8 1.3 copy-start.15
  49.9 29.5 %copy-start.6 = (f32[1,8,32,256]{3,2,1,0:T(8,128)}, f32[1,8,32,256]{3,2,1,0:T(8,128)S(1)}, u32[]{:S(2)}) copy-start(f32[1,8,32,256]{3,2,1,0:T(8,128)S(1)} %get-tuple-element.71) | copy-start | bytes 786436
  49.9 29.5 %copy-start.8 = (f32[1,8,32,256]{3,2,1,0:T(8,128)}, f32[1,8,32,256]{3,2,1,0:T(8,128)S(1)}, u32[]{:S(2)}) copy-start(f32[1,8,32,256]{3,2,1,0:T(8,128)S(1)} %get-tuple-element.72) | copy-start | bytes 786436
  50.0 29.5 %copy-start.10 = (f32[1,8,32,256]{3,2,1,0:T(8,128)}, f32[1,8,32,256]{3,2,1,0:T(8,128)S(1)}, u32[]{:S(2)}) copy-start(f32[1,8,32,256]{3,2,1,0:T(8,128)S(1)} %get-tuple-element.73) | copy-start | bytes 786436
  50.1 30.2 %copy-start.2 = (f32[3,8,32,256]{3,2,1,0:T(8,128)}, f32[3,8,32,256]{3,2,1,0:T(8,128)S(1)}, u32[]{:S(2)}) copy-start(f32[3,8,32,256]{3,2,1,0:T(8,128)S(1)} %fusion.4) | copy-start | bytes 2359300
  80.3 9.7 %collective-permute-start.6 = (f32[4,2,32,256]{3,2,1,0:T(8,128)}, f32[4,2,32,256]{3,2,1,0:T(8,128)S(1)}, u32[]{:S(2)}, u32[]{:S(2)}) collective-permute-start(f32[4,2,32,256]{3,2,1,0:T(8,128)} %get-tuple-element.64), channel_id=1, source_target_pairs={{0,4},{4,8},{8,12},{1,5},{5,9},{9,13},{2,6},{6,10},{10,14},{3,7},{... | collective-permute-start | bytes 786440 | tf_op jit(solution)/shard_map/ppermute | solution.py:21
  83.8 10.9 %collective-permute-start.7 = (f32[4,2,32,256]{3,2,1,0:T(8,128)}, f32[4,2,32,256]{3,2,1,0:T(8,128)}, u32[]{:S(2)}, u32[]{:S(2)}) collective-permute-start(f32[4,2,32,256]{3,2,1,0:T(8,128)} %get-tuple-element.65), channel_id=1, source_target_pairs={{4,0},{8,4},{12,8},{5,1},{9,5},{13,9},{6,2},{10,6},{14,10},{7,3},{... | collective-permute-start | bytes 786440 | tf_op jit(solution)/shard_map/ppermute | solution.py:24
  95.9 4.1 %collective-permute-start.8 = (f32[4,12,2,256]{3,2,1,0:T(2,128)S(1)}, f32[4,12,2,256]{3,2,1,0:T(2,128)S(1)}, u32[]{:S(2)}, u32[]{:S(2)}) collective-permute-start(f32[4,12,2,256]{3,2,1,0:T(2,128)S(1)} %get-tuple-element.56), channel_id=1, source_target_pairs={{0,2},{1,3},{4,6},{5,7},{8,10},{9,11},{12,14},{13,15},{16,18},{17,... | collective-permute-start | bytes 294920 | tf_op jit(solution)/shard_map/ppermute | solution.py:21
  97.4 6.7 %collective-permute-start.9 = (f32[4,12,2,256]{3,2,1,0:T(2,128)S(1)}, f32[4,12,2,256]{3,2,1,0:T(2,128)S(1)}, u32[]{:S(2)}, u32[]{:S(2)}) collective-permute-start(f32[4,12,2,256]{3,2,1,0:T(2,128)S(1)} %get-tuple-element.57), channel_id=1, source_target_pairs={{2,0},{3,1},{6,4},{7,5},{10,8},{11,9},{14,12},{15,13},{18,16},{19,... | collective-permute-start | bytes 294920 | tf_op jit(solution)/shard_map/ppermute | solution.py:24
  104.1 3.1 %copy-start.12 = (f32[4,12,2,256]{3,2,1,0:T(2,128)}, f32[4,12,2,256]{3,2,1,0:T(2,128)S(1)}, u32[]{:S(2)}) copy-start(f32[4,12,2,256]{3,2,1,0:T(2,128)S(1)} %collective-permute-done.9) | copy-start | bytes 294916
  108.8 8.1 %collective-permute-start.10 = (f32[4,12,36,2]{2,0,3,1:T(4,128)S(1)}, f32[4,12,36,2]{2,0,3,1:T(4,128)}, u32[]{:S(2)}, u32[]{:S(2)}) collective-permute-start(f32[4,12,36,2]{2,0,3,1:T(4,128)S(1)} %copy.28), channel_id=1, source_target_pairs={{0,1},{2,3},{4,5},{6,7},{8,9},{10,11},{12,13},{14,15},{16,17},{18,... | collective-permute-start | bytes 41480 | tf_op jit(solution)/shard_map/ppermute | solution.py:21
  113.0 6.2 %collective-permute-start.11 = (f32[4,12,36,2]{2,0,3,1:T(4,128)}, f32[4,12,36,2]{2,0,3,1:T(4,128)}, u32[]{:S(2)}, u32[]{:S(2)}) collective-permute-start(f32[4,12,36,2]{2,0,3,1:T(4,128)} %copy.29), channel_id=1, source_target_pairs={{1,0},{3,2},{5,4},{7,6},{9,8},{11,10},{13,12},{15,14},{17,16},{19,... | collective-permute-start | bytes 41480 | tf_op jit(solution)/shard_map/ppermute | solution.py:24
  124.9 3.8 %copy-start.3 = (f32[12,36,260]{2,1,0:T(8,128)}, f32[12,36,260]{2,1,0:T(8,128)S(1)}, u32[]{:S(2)}) copy-start(f32[12,36,260]{2,1,0:T(8,128)S(1)} %get-tuple-element.33) | copy-start | bytes 1347844
  130.8 1.2 copy-start.7
  130.8 1.2 copy-start.9
  130.8 1.2 copy-start.11
  132.0 1.6 copy-start.14
  132.0 1.6 copy-start.16
  133.1 62.5 %copy-start.4 = (f32[12,36,260]{2,1,0:T(8,128)S(1)}, f32[12,36,260]{2,1,0:T(8,128)}, u32[]{:S(2)}) copy-start(f32[12,36,260]{2,1,0:T(8,128)} %copy-done.3) | copy-start | bytes 1347844
where the time goes:
time: 228 us; the launch traced here: 227 us
  other arithmetic  89.2 us (39%)
  blocking collectives  60.5 us (27%)
  waiting for transfers between devices  27.4 us (12%)
  starting transfers between devices  24.9 us (11%)
  local copies, waits for them, and re-layouts  21.7 us (10%)
    psum x1, blocking collectives, local(): readings = lax.psum(partial_sum, ('slab', 'pencil', 'comp'))  60.5 us
    add x1, other arithmetic, advance(): damage_core + TIME_DAMAGE * (2.0 * (1.0 - damage_core) * energy - toughne...  31 us
    broadcast_in_dim x2, other arithmetic, local(): stacked = jnp.concatenate([moved, damage[None]], axis=0)  30.5 us
    ppermute x6, waiting for transfers between devices, with_halo(): lax.ppermute(lax.slice_in_dim(block, 0, width, axis=dim), axis, backward)  17.3 us
    ppermute x6, starting transfers between devices, with_halo(): lax.ppermute(lax.slice_in_dim(block, block.shape[dim] - width, None, axis...  17.2 us
    ppermute x6, waiting for transfers between devices, with_halo(): lax.ppermute(lax.slice_in_dim(block, block.shape[dim] - width, None, axis...  10.2 us
    mul x4, other arithmetic, advance(): total_force = total_force + central(degrade * stress, direction)  9.3 us
    concatenate x4, other arithmetic, with_halo(): block = jnp.concatenate([low, block, high], axis=dim)  8.23 us
  transfers between devices with their start and end apart: 12, of which 8 were waited for; matrix products, arithmetic and copies ran while one was open for 6% of the time, Pallas kernels for 0%

commit v1 on v0

v1 whole, which is shorter than its diff:
```python
import itertools

import jax
import jax.numpy as jnp
import numpy as np
from jax import lax
from jax.experimental import pallas as pl
from jax.experimental.pallas import tpu as pltpu
from jax.sharding import PartitionSpec as P

RESIDUAL_STIFF = 0.001
TIME_DISP = 0.15
TIME_DAMAGE = 0.08
DAMAGE_LEVEL = 0.45
POINT_GAIN = 8.0
AXES = ("slab", "pencil", "comp")
MESH = pl.DeviceIdType.MESH
F32 = jnp.float32


def third_angle_poly():
    nodes = 0.5 + 0.5 * np.cos(np.pi * (np.arange(200) + 0.5) / 200)
    fit = np.polynomial.chebyshev.Chebyshev.fit(
        nodes, np.cos(np.arccos(nodes) / 3.0), 8, domain=[0.0, 1.0]
    )
    return [float(c) for c in fit.convert(kind=np.polynomial.Polynomial).coef]


POLY = third_angle_poly()

DIRECTIONS = [
    d for d in itertools.product((-1, 0, 1), repeat=3) if 1 <= sum(map(abs, d)) <= 2
]
FAST = [d for d in DIRECTIONS if d[0] == 0]
SLOW = [d for d in DIRECTIONS if d[0] != 0]


def energy_of(e00, e11, e22, e01, e02, e12):
    trace = e00 + e11 + e22
    mean = trace * (1.0 / 3.0)
    d0, d1, d2 = e00 - mean, e11 - mean, e22 - mean
    p2 = (d0 * d0 + d1 * d1 + d2 * d2) * (1.0 / 6.0) + (
        e01 * e01 + e02 * e02 + e12 * e12
    ) * (1.0 / 3.0)
    inv = lax.rsqrt(jnp.maximum(p2, 1e-36))
    p = p2 * inv
    b0, b1, b2 = d0 * inv, d1 * inv, d2 * inv
    b01, b02, b12 = e01 * inv, e02 * inv, e12 * inv
    half_det = 0.5 * (
        b0 * (b1 * b2 - b12 * b12)
        - b01 * (b01 * b2 - b12 * b02)
        + b02 * (b01 * b12 - b1 * b02)
    )
    r = jnp.minimum(jnp.abs(half_det), 1.0)
    c = jnp.full_like(r, POLY[-1])
    for coefficient in POLY[-2::-1]:
        c = c * r + coefficient
    tc = p * c
    t = jnp.where(half_det < 0.0, -tc, tc)
    s2 = jnp.maximum(1.0 - c * c, 0.0)
    delta = p * (s2 * lax.rsqrt(jnp.maximum(s2, 1e-30))) * float(np.sqrt(3.0))
    f1 = jnp.maximum(mean + 2.0 * t, 0.0)
    f2 = jnp.maximum(mean - t + delta, 0.0)
    f3 = jnp.maximum(mean - t - delta, 0.0)
    ft = jnp.maximum(trace, 0.0)
    return 0.75 * ft * ft + f1 * f1 + f2 * f2 + f3 * f3


def make_kernel(planes, rows, columns, sensors, sizes, owners):
    n_slab, n_pencil, n_comp = sizes
    count = n_slab * n_pencil * n_comp
    Z, R, C = planes, rows, columns
    piece = sensors // owners
    half = piece // 2

    def kernel(u_hbm, tough_hbm, crack_hbm, weight_hbm, cell_ref,
               moved_ref, damage_ref, read_ref,
               U, XR, YR, YP, YXR, TZ, tough, crack, weight, pooled_t, hot, partial, RB, GB,
               in_sem, send_sem, recv_sem, rs_send, rs_recv, ag_send, ag_recv):
        me = [lax.axis_index(a) for a in AXES]
        flat = (me[0] * n_pencil + me[1]) * n_comp + me[2]

        def device(index):
            return {
                "slab": index // (n_pencil * n_comp),
                "pencil": (index // n_comp) % n_pencil,
                "comp": index % n_comp,
            }

        loads = [
            pltpu.make_async_copy(u_hbm, U.at[0, 0:3, 2:Z + 2, 0:R, 0:C], in_sem.at[0]),
            pltpu.make_async_copy(crack_hbm, crack, in_sem.at[1]),
            pltpu.make_async_copy(tough_hbm, tough, in_sem.at[2]),
            pltpu.make_async_copy(weight_hbm, weight, in_sem.at[3]),
        ]
        for load in loads:
            load.start()

        for step in range(2):
            for z in (0, 1, Z + 2, Z + 3):
                U[step, :, z, 0:R, 0:C] = jnp.zeros((4, R, C), F32)
        XR[...] = jnp.zeros(XR.shape, F32)
        YR[...] = jnp.zeros(YR.shape, F32)
        YXR[...] = jnp.zeros(YXR.shape, F32)

        barrier = pltpu.get_barrier_semaphore()

        def greet(k, carry):
            pl.semaphore_signal(
                barrier, inc=1, device_id=device((flat + k) % count), device_id_type=MESH
            )
            return carry

        lax.fori_loop(1, count, greet, 0)
        pl.semaphore_wait(barrier, count - 1)

        loads[1].wait()

        def label(z, carry):
            U[0, 3, z + 2, 0:R, 0:C] = DAMAGE_LEVEL * crack[z].astype(F32)
            return carry

        lax.fori_loop(0, Z, label, 0)
        loads[0].wait()

        def copies(step, d):
            dz, dy, dx = d
            sy, sx = (dy + 1) // 2, (dx + 1) // 2
            lanes = slice(C - 128, C) if dx > 0 else slice(0, 128)
            edge = Z - 1 if dz > 0 else 0
            halo = 0 if dz > 0 else Z + 1
            if dz and not dy and not dx:
                first = Z if dz > 0 else 2
                target = 0 if dz > 0 else Z + 2
                pairs = [
                    (U.at[step, 0:3, first:first + 2, 0:R, 0:C],
                     U.at[step, 0:3, target:target + 2, 0:R, 0:C]),
                    (U.at[step, 3, edge + 2, 0:R, 0:C], U.at[step, 3, halo + 1, 0:R, 0:C]),
                ]
            elif dz and dy:
                pairs = [(YP.at[step, sy, edge], YR.at[step, 1 - sy, halo])]
            elif dz and dx:
                pairs = [(U.at[step, 0:3, edge + 2, 0:R, lanes], XR.at[step, 1 - sx, 0:3, halo])]
            elif dy and dx:
                pairs = [(YP.at[step, sy, :, :, lanes], YXR.at[step, 1 - sy, 1 - sx])]
            elif dy:
                pairs = [(YP.at[step, sy], YR.at[step, 1 - sy, 1:Z + 1])]
            else:
                pairs = [(U.at[step, :, 2:Z + 2, 0:R, lanes], XR.at[step, 1 - sx, :, 1:Z + 1])]
            index = DIRECTIONS.index(d)
            return [
                pltpu.make_async_remote_copy(
                    src_ref=src,
                    dst_ref=dst,
                    send_sem=send_sem.at[step, index, k],
                    recv_sem=recv_sem.at[step, index, k],
                    device_id={a: m + o for a, m, o in zip(AXES, me, d)},
                    device_id_type=MESH,
                )
                for k, (src, dst) in enumerate(pairs)
            ]

        def inside(d, sign):
            ok = None
            for m, o, n in zip(me, d, sizes):
                if o:
                    here = m + 1 < n if sign * o > 0 else m >= 1
                    ok = here if ok is None else jnp.logical_and(ok, here)
            return ok

        def feasible(d):
            return all(n > 1 for o, n in zip(d, sizes) if o)

        def each(step, directions, sign, action):
            for d in directions:
                if feasible(d):
                    @pl.when(inside(d, sign))
                    def _():
                        for copy in copies(step, d):
                            action(copy)

        row8 = lax.broadcasted_iota(jnp.int32, (8, C), 0)
        row8t = lax.broadcasted_iota(jnp.int32, (8, 128), 0)
        lane8 = lax.broadcasted_iota(jnp.int32, (8, 128), 1)
        lane_r = lax.broadcasted_iota(jnp.int32, (R, 128), 1)

        def roll(value, shift, axis):
            shift = shift % value.shape[axis]
            return pltpu.roll(value, shift, axis) if shift else value

        def pack(step):
            def one(z, carry):
                low = [U[step, f, z + 2, 0:8, 0:C] for f in range(4)]
                high = [U[step, f, z + 2, R - 8:R, 0:C] for f in range(4)]
                for side, tiles, shifts in (
                    (0, low, (0, 2, 4, 6)), (1, high, (2, 4, 6, 7))
                ):
                    rolled = [roll(t, s, 0) for t, s in zip(tiles, shifts)]
                    YP[step, side, z] = jnp.where(
                        row8 < 2, rolled[0],
                        jnp.where(row8 < 4, rolled[1], jnp.where(row8 < 6, rolled[2], rolled[3])),
                    )
                return carry

            lax.fori_loop(0, Z, one, 0)

        def merged(low, high, f, row):
            up, down = ((8 - 2 * f) % 8, 6 - 2 * f) if f < 3 else (2, 1)
            return jnp.where(row < 4, roll(high, up, 0), roll(low, down, 0))

        def unpack(step, z, full):
            fields = range(4 if full else 3)
            low, high = YR[step, 0, z + 1], YR[step, 1, z + 1]
            for f in fields:
                U[step, f, z + 2, R:R + 8, 0:C] = merged(low, high, f, row8)
                U[step, f, z + 2, 0:R, C:C + 128] = jnp.where(
                    lane_r < 64, XR[step, 1, f, z + 1], XR[step, 0, f, z + 1]
                )
            if full:
                left, right = [
                    [YXR[step, sy, sx, z] for sy in range(2)] for sx in range(2)
                ]
                for f in range(3):
                    U[step, f, z + 2, R:R + 8, C:C + 128] = jnp.where(
                        lane8 < 64, merged(*right, f, row8t), merged(*left, f, row8t)
                    )

        def ends(step, z):
            now = [U[step, i, z + 2] for i in range(3)]
            gz = [
                U[step, i, z + 3, 0:R, 0:C] - U[step, i, z + 1, 0:R, 0:C] for i in range(3)
            ]

            def along(value, axis):
                return (roll(value, -1, axis) - roll(value, 1, axis))[0:R, 0:C]

            gy0, gy1 = along(now[0], 0), along(now[1], 0)
            gx0, gx2 = along(now[0], 1), along(now[2], 1)
            keep = 1.0 - U[step, 3, z + 2, 0:R, 0:C]
            g = (0.5 * TIME_DISP) * (keep * keep + RESIDUAL_STIFF)
            TZ[z + 1, 0] = g * (gz[0] + 0.75 * (gz[0] + gy1 + gx2))
            TZ[z + 1, 1] = g * (0.5 * (gz[1] + gy0))
            TZ[z + 1, 2] = g * (0.5 * (gz[2] + gx0))

        def store(step, f, z, value):
            if step == 0:
                U[1, f, z + 2, 0:R, 0:C] = value
            elif f < 3:
                moved_ref[f, z] = value
            else:
                damage_ref[z] = value

        def load(step, f, z):
            return U[1, f, z + 2, 0:R, 0:C] if step == 0 else moved_ref[f, z]

        def body(step, z):
            now = [U[step, i, z + 2] for i in range(3)]
            gz = [U[step, i, z + 3] - U[step, i, z + 1] for i in range(3)]
            gy = [roll(v, -1, 0) - roll(v, 1, 0) for v in now]
            gx = [roll(v, -1, 1) - roll(v, 1, 1) for v in now]
            d = U[step, 3, z + 2]
            keep = 1.0 - d
            g = (0.5 * TIME_DISP) * (keep * keep + RESIDUAL_STIFF)
            lam = 0.75 * (gz[0] + gy[1] + gx[2])
            s01 = 0.5 * (gz[1] + gy[0])
            s02 = 0.5 * (gz[2] + gx[0])
            s12 = 0.5 * (gy[2] + gx[1])
            in_y = [g * s01, g * (gy[1] + lam), g * s12]
            in_x = [(g * s02)[0:R], in_y[2][0:R], (g * (gx[2] + lam))[0:R]]
            TZ[z + 1, 0] = (g * (gz[0] + lam))[0:R, 0:C]
            TZ[z + 1, 1] = in_y[0][0:R, 0:C]
            TZ[z + 1, 2] = in_x[0][:, 0:C]
            for i in range(3):
                ty = in_y[i][:, 0:C]
                force = (roll(ty, -1, 0) - roll(ty, 1, 0))[0:R] + (
                    roll(in_x[i], -1, 1) - roll(in_x[i], 1, 1)
                )[:, 0:C]
                store(step, i, z, now[i][0:R, 0:C] + force)

            def core(value):
                return value[0:R, 0:C]

            energy = energy_of(
                0.5 * core(gz[0]), 0.5 * core(gy[1]), 0.5 * core(gx[2]),
                0.5 * core(s01), 0.5 * core(s02), 0.5 * core(s12),
            )
            dy = d[:, 0:C]
            dx = d[0:R]
            dc = core(d)
            lap = (
                U[step, 3, z + 3, 0:R, 0:C] + U[step, 3, z + 1, 0:R, 0:C]
                + (roll(dy, -1, 0) + roll(dy, 1, 0))[0:R]
                + (roll(dx, -1, 1) + roll(dx, 1, 1))[:, 0:C]
                - 6.0 * dc
            )
            store(step, 3, z, dc + TIME_DAMAGE * (
                2.0 * (1.0 - dc) * energy + tough[z] * (lap - dc)
            ))

        def finish(step, z):
            for i in range(3):
                store(step, i, z, load(step, i, z) + (TZ[z + 2, i] - TZ[z, i]))

        def loop(start, stop, function):
            def one(z, carry):
                function(z)
                return carry

            lax.fori_loop(start, stop, one, 0)

        for step in range(2):
            pack(step)
            each(step, SLOW, 1, lambda copy: copy.start())
            each(step, FAST, 1, lambda copy: copy.start())
            if step == 0:
                loads[2].wait()
                base = me[0] * Z * (R * n_pencil) + me[1] * R
                row_id = lax.broadcasted_iota(jnp.int32, (R, 512), 0) * n_comp

                def choose(z, carry):
                    start = (base + z * (R * n_pencil)) * n_comp + me[2]
                    for s in range(0, sensors, 512):
                        hit = row_id == cell_ref[:, s:s + 512] - start
                        hot[z, :, s:s + 512] = jnp.where(hit, POINT_GAIN, 0.0).astype(jnp.bfloat16)
                    return carry

                lax.fori_loop(0, Z, choose, 0)
            each(step, FAST, -1, lambda copy: copy.wait_recv())
            loop(0, Z, lambda z: unpack(step, z, True))
            loop(1, Z - 1, lambda z: body(step, z))
            each(step, SLOW, -1, lambda copy: copy.wait_recv())
            unpack(step, -1, False)
            unpack(step, Z, False)
            loop(0, 2, lambda k: body(step, k * (Z - 1)))
            loop(0, 2, lambda k: ends(step, k * (Z + 1) - 1))
            loop(0, Z, lambda z: finish(step, z))
            each(step, SLOW, 1, lambda copy: copy.wait_send())
            each(step, FAST, 1, lambda copy: copy.wait_send())

        def pool(z):
            total = jnp.zeros((R, 128), F32)
            for i in range(3):
                mean = jnp.sum(moved_ref[i, z], axis=1, keepdims=True) * (1.0 / C)
                total = jnp.where(lane_r == i, mean, total)
            pooled_t[pl.ds(pl.multiple_of(z * R, R), R), :] = total

        loop(0, Z, pool)
        pooled = pooled_t[...].T[0:8].astype(jnp.bfloat16)
        loads[3].wait()
        chunk = piece
        for q in range(owners):
            for h in range(2):
                s = q * piece + h * half
                value = jnp.dot(
                    pooled, weight[:, s:s + half], preferred_element_type=F32
                ) + jnp.dot(
                    pooled, hot[:, :, s:s + half].reshape(Z * R, half), preferred_element_type=F32
                )
                partial[q, 4 * h:4 * h + 4] = value[0:4]

        def scatter(q):
            return pltpu.make_async_remote_copy(
                src_ref=partial.at[q], dst_ref=RB.at[flat],
                send_sem=rs_send.at[q], recv_sem=rs_recv.at[flat],
                device_id=device(q), device_id_type=MESH,
            )

        def scatter_from(k):
            return pltpu.make_async_remote_copy(
                src_ref=partial.at[0], dst_ref=RB.at[k],
                send_sem=rs_send.at[0], recv_sem=rs_recv.at[k],
                device_id=device(k), device_id_type=MESH,
            )

        def gather(q, k):
            return pltpu.make_async_remote_copy(
                src_ref=GB.at[q], dst_ref=GB.at[q],
                send_sem=ag_send.at[k], recv_sem=ag_recv.at[q],
                device_id=device(k), device_id_type=MESH,
            )

        def others(stop, function):
            def one(k):
                @pl.when(k != flat)
                def _():
                    function(k)

            loop(0, stop, one)

        others(owners, lambda q: scatter(q).start())

        @pl.when(flat < owners)
        def _():
            others(count, lambda k: scatter_from(k).wait_recv())
            RB[flat] = partial[flat]

            def add(k, total):
                return total + RB[k]

            GB[flat] = lax.fori_loop(1, count, add, RB[0])
            others(count, lambda k: gather(flat, k).start())

        others(owners, lambda q: gather(q, 0).wait_recv())
        for q in range(owners):
            read_ref[:, q * piece:q * piece + half] = GB[q, 0:3]
            read_ref[:, q * piece + half:(q + 1) * piece] = GB[q, 4:7]
        others(owners, lambda q: scatter(q).wait_send())

        @pl.when(flat < owners)
        def _():
            others(count, lambda k: gather(flat, k).wait_send())

    return kernel


def solution(mesh):
    sizes = tuple(mesh.shape[a] for a in AXES)
    count = sizes[0] * sizes[1] * sizes[2]

    def local(u_start, toughness, crack_label, obs_weight, sensor_cell):
        Z, R, C = toughness.shape
        S = sensor_cell.shape[0]
        owners = 1
        while owners * 2 <= count and S % (owners * 512) == 0:
            owners *= 2
        piece = S // owners
        n_dir = len(DIRECTIONS)
        any_spec = pl.BlockSpec(memory_space=pl.ANY)
        vmem_spec = pl.BlockSpec(memory_space=pltpu.VMEM)
        dma = pltpu.SemaphoreType.DMA
        return pl.pallas_call(
            make_kernel(Z, R, C, S, sizes, owners),
            out_shape=(
                jax.ShapeDtypeStruct((3, Z, R, C), F32),
                jax.ShapeDtypeStruct((Z, R, C), F32),
                jax.ShapeDtypeStruct((3, S), F32),
            ),
            in_specs=[any_spec] * 4 + [vmem_spec],
            out_specs=[vmem_spec] * 3,
            scratch_shapes=[
                pltpu.VMEM((2, 4, Z + 4, R + 8, C + 128), F32),
                pltpu.VMEM((2, 2, 4, Z + 2, R, 128), F32),
                pltpu.VMEM((2, 2, Z + 2, 8, C), F32),
                pltpu.VMEM((2, 2, Z, 8, C), F32),
                pltpu.VMEM((2, 2, 2, Z, 8, 128), F32),
                pltpu.VMEM((Z + 2, 3, R, C), F32),
                pltpu.VMEM((Z, R, C), F32),
                pltpu.VMEM((Z, R, C), jnp.int32),
                pltpu.VMEM((Z * R, S), jnp.bfloat16),
                pltpu.VMEM((Z * R, 128), F32),
                pltpu.VMEM((Z, R, S), jnp.bfloat16),
                pltpu.VMEM((owners, 8, piece // 2), F32),
                pltpu.VMEM((count, 8, piece // 2), F32),
                pltpu.VMEM((owners, 8, piece // 2), F32),
                dma((4,)),
                dma((2, n_dir, 2)),
                dma((2, n_dir, 2)),
                dma((owners,)),
                dma((count,)),
                dma((count,)),
                dma((owners,)),
            ],
            compiler_params=pltpu.CompilerParams(
                collective_id=0, has_side_effects=True, vmem_limit_bytes=60 * 1024 * 1024
            ),
            name="fracture",
        )(
            u_start, toughness, crack_label,
            obs_weight.reshape(Z * R, S), sensor_cell.reshape(1, S),
        )

    return jax.shard_map(
        local,
        mesh=mesh,
        in_specs=(
            P(None, ("groups", "slab"), "pencil", "comp"),
            P(("groups", "slab"), "pencil", "comp"),
            P(("groups", "slab"), "pencil", "comp"),
            P("slab", "pencil", "comp", None),
            P(),
        ),
        out_specs=(
            P(None, ("groups", "slab"), "pencil", "comp"),
            P(("groups", "slab"), "pencil", "comp"),
            P(None, "groups"),
        ),
        check_vma=False,
    )
```

time: 228 us -> 44.1 us (0.19)
  other arithmetic: 89.2 us -> 0 us
  blocking collectives: 60.5 us -> 0 us
  Pallas kernels: 0 us -> 38.8 us
  waiting for transfers between devices: 27.4 us -> 0 us
  starting transfers between devices: 24.9 us -> 0 us
  local copies, waits for them, and re-layouts: 21.7 us -> 4.42 us
    psum x1 -> x0, blocking collectives: 60.5 us -> none  [local(): readings = lax.psum(partial_sum, ('slab', 'pencil', 'comp'))]
    pallas_call x0 -> x1, Pallas kernels: none -> 38.8 us  [local(): pl.pallas_call(make_kernel(Z, R, C, S, sizes, owners), out_shape=(jax.Sha...]
    add x4 -> x0, other arithmetic: 33 us -> none  [the longest x1 31 us: advance(): damage_core + TIME_DAMAGE * (2.0 * (1.0 - damage_core) * energy - toughne...]
    broadcast_in_dim x2 -> x0, other arithmetic: 30.5 us -> none  [local(): stacked = jnp.concatenate([moved, damage[None]], axis=0)]
    ppermute x12 -> x0, waiting for transfers between devices: 27.4 us -> none  [the longest x6 17.3 us: with_halo(): lax.ppermute(lax.slice_in_dim(block, 0, width, axis=dim), axis, backward)]
    ppermute x12 -> x0, starting transfers between devices: 24.9 us -> none  [the longest x6 17.2 us: with_halo(): lax.ppermute(lax.slice_in_dim(block, block.shape[dim] - width, None, axis...]
    slice x6 -> x0, local copies, waits for them, and re-layouts: 11 us -> none  [the longest x4 6.5 us: with_halo(): lax.slice_in_dim(block, block.shape[dim] - width, None, axis=dim)]
    mul x5 -> x0, other arithmetic: 9.87 us -> none  [the longest x4 9.3 us: advance(): total_force = total_force + central(degrade * stress, direction)]
  transfers between devices with their start and end apart: 12 -> 0, of which waited for: 8 -> 0; matrix products, arithmetic and copies ran while one was open for 6% -> 0% of each run, Pallas kernels for 0% -> 0%
where the time goes in v1:
time: 44.1 us; the launch traced here: 43.9 us
  Pallas kernels  38.8 us (88%)
  local copies, waits for them, and re-layouts  4.42 us (10%)
  between operations  0.65 us (1%)
    pallas_call x1, Pallas kernels, local(): pl.pallas_call(make_kernel(Z, R, C, S, sizes, owners), out_shape=(jax.Sha...  38.8 us
    unnamed x5, local copies, waits for them, and re-layouts  4.42 us

profile of v1, /device:TPU:0, one launch (start us, length us, event | category | flops | bytes accessed | tf_op | source)
XLA Modules:
  0.0 43.9 jit_solution(2908206728756523103)
XLA Ops:
  0.6 38.8 %fracture.1 = (f32[3,8,32,256]{3,2,1,0:T(8,128)}, f32[8,32,256]{2,1,0:T(8,128)}, f32[3,4096]{1,0:T(4,128)}) custom-call(f32[3,8,32,256]{3,2,1,0:T(8,128)} %u_hbm.1, f32[8,32,256]{2,1,0:T(8,128)} %tough_hbm.1, s32[8,32,256]{2,1,0:T(8,128)} %crack_hbm.1, bf16[256,4096]{1,0:T(8,128)(2,1)} %bitcast.2, s32[1,4096]{1,0:T(1,128)} %bitcast.3), custom_call_target="tpu_custom_call" | custom-call | tf_op jit(solution)/shard_map/fracture/pallas_call | solution.py:431
  39.4 0.0 copy-start
  39.5 2.1 %copy.11 = f32[3,8,32,256]{3,2,1,0:T(8,128)} copy(f32[3,8,32,256]{3,2,1,0:T(8,128)} %get-tuple-element.6) | data formatting | bytes 1572864
  41.6 1.7 %copy.12 = f32[8,32,256]{2,1,0:T(8,128)} copy(f32[8,32,256]{2,1,0:T(8,128)} %get-tuple-element.7) | data formatting | bytes 524288
  43.2 0.0 copy-done
  43.2 0.6 %copy.13 = f32[3,4096]{1,0:T(4,128)} copy(f32[3,4096]{1,0:T(4,128)S(1)} %copy-done) | data formatting | bytes 98304
Async XLA Ops:
  39.4 3.8 %copy-start = (f32[3,4096]{1,0:T(4,128)S(1)}, f32[3,4096]{1,0:T(4,128)}, u32[]{:S(2)}) copy-start(f32[3,4096]{1,0:T(4,128)} %get-tuple-element.8) | copy-start | bytes 147460

commit v2 on v1

--- a/solution.py
+++ b/solution.py
@@ -31,7 +31,10 @@
 DIRECTIONS = [
     d for d in itertools.product((-1, 0, 1), repeat=3) if 1 <= sum(map(abs, d)) <= 2
 ]
-FAST = [d for d in DIRECTIONS if d[0] == 0]
+FAST_X = [d for d in DIRECTIONS if d[0] == 0 and d[1] == 0]
+FAST_Y = [d for d in DIRECTIONS if d[0] == 0 and d[1] != 0]
+FACES = [(0, 0, -1), (0, 0, 1), (-1, 0, 0), (1, 0, 0), (0, -1, 0), (0, 1, 0)]
+ORDER = FACES + [d for d in FAST_Y if d[2]] + [d for d in DIRECTIONS if d[0] and (d[1] or d[2])]
 SLOW = [d for d in DIRECTIONS if d[0] != 0]
 
 
@@ -208,15 +211,17 @@
             up, down = ((8 - 2 * f) % 8, 6 - 2 * f) if f < 3 else (2, 1)
             return jnp.where(row < 4, roll(high, up, 0), roll(low, down, 0))
 
-        def unpack(step, z, full):
-            fields = range(4 if full else 3)
-            low, high = YR[step, 0, z + 1], YR[step, 1, z + 1]
-            for f in fields:
-                U[step, f, z + 2, R:R + 8, 0:C] = merged(low, high, f, row8)
+        def unpack_x(step, z, fields):
+            for f in range(fields):
                 U[step, f, z + 2, 0:R, C:C + 128] = jnp.where(
                     lane_r < 64, XR[step, 1, f, z + 1], XR[step, 0, f, z + 1]
                 )
-            if full:
+
+        def unpack_y(step, z, fields):
+            low, high = YR[step, 0, z + 1], YR[step, 1, z + 1]
+            for f in range(fields):
+                U[step, f, z + 2, R:R + 8, 0:C] = merged(low, high, f, row8)
+            if fields == 4:
                 left, right = [
                     [YXR[step, sy, sx, z] for sy in range(2)] for sx in range(2)
                 ]
@@ -310,8 +315,7 @@
 
         for step in range(2):
             pack(step)
-            each(step, SLOW, 1, lambda copy: copy.start())
-            each(step, FAST, 1, lambda copy: copy.start())
+            each(step, ORDER, 1, lambda copy: copy.start())
             if step == 0:
                 loads[2].wait()
                 base = me[0] * Z * (R * n_pencil) + me[1] * R
@@ -325,17 +329,19 @@
                     return carry
 
                 lax.fori_loop(0, Z, choose, 0)
-            each(step, FAST, -1, lambda copy: copy.wait_recv())
-            loop(0, Z, lambda z: unpack(step, z, True))
+            each(step, FAST_X, -1, lambda copy: copy.wait_recv())
+            loop(0, Z, lambda z: unpack_x(step, z, 4))
+            each(step, FAST_Y, -1, lambda copy: copy.wait_recv())
+            loop(0, Z, lambda z: unpack_y(step, z, 4))
             loop(1, Z - 1, lambda z: body(step, z))
             each(step, SLOW, -1, lambda copy: copy.wait_recv())
-            unpack(step, -1, False)
-            unpack(step, Z, False)
+            for z in (-1, Z):
+                unpack_x(step, z, 3)
+                unpack_y(step, z, 3)
             loop(0, 2, lambda k: body(step, k * (Z - 1)))
             loop(0, 2, lambda k: ends(step, k * (Z + 1) - 1))
             loop(0, Z, lambda z: finish(step, z))
-            each(step, SLOW, 1, lambda copy: copy.wait_send())
-            each(step, FAST, 1, lambda copy: copy.wait_send())
+            each(step, ORDER, 1, lambda copy: copy.wait_send())
 
         def pool(z):
             total = jnp.zeros((R, 128), F32)
@@ -347,17 +353,6 @@
         loop(0, Z, pool)
         pooled = pooled_t[...].T[0:8].astype(jnp.bfloat16)
         loads[3].wait()
-        chunk = piece
-        for q in range(owners):
-            for h in range(2):
-                s = q * piece + h * half
-                value = jnp.dot(
-                    pooled, weight[:, s:s + half], preferred_element_type=F32
-                ) + jnp.dot(
-                    pooled, hot[:, :, s:s + half].reshape(Z * R, half), preferred_element_type=F32
-                )
-                partial[q, 4 * h:4 * h + 4] = value[0:4]
-
         def scatter(q):
             return pltpu.make_async_remote_copy(
                 src_ref=partial.at[q], dst_ref=RB.at[flat],
@@ -387,7 +382,25 @@
 
             loop(0, stop, one)
 
-        others(owners, lambda q: scatter(q).start())
+        for q in range(owners):
+            for h in range(2):
+                cut = q * piece + h * half
+                value = jnp.dot(
+                    pooled, weight[:, cut:cut + half], preferred_element_type=F32
+                ) + jnp.dot(
+                    pooled, hot[:, :, cut:cut + half].reshape(Z * R, half),
+                    preferred_element_type=F32,
+                )
+                partial[q, 4 * h:4 * h + 4] = value[0:4]
+
+        def send(k):
+            q = (flat + k) % count
+
+            @pl.when(q < owners)
+            def _():
+                scatter(q).start()
+
+        loop(1, count, send)
 
         @pl.when(flat < owners)
         def _():
@@ -398,7 +411,7 @@
                 return total + RB[k]
 
             GB[flat] = lax.fori_loop(1, count, add, RB[0])
-            others(count, lambda k: gather(flat, k).start())
+            loop(1, count, lambda k: gather(flat, (flat + k) % count).start())
 
         others(owners, lambda q: gather(q, 0).wait_recv())
         for q in range(owners):
@@ -425,7 +438,7 @@
             owners *= 2
         piece = S // owners
         n_dir = len(DIRECTIONS)
-        any_spec = pl.BlockSpec(memory_space=pl.ANY)
+        any_spec = pl.BlockSpec(memory_space=pltpu.HBM)
         vmem_spec = pl.BlockSpec(memory_space=pltpu.VMEM)
         dma = pltpu.SemaphoreType.DMA
         return pl.pallas_call(
@@ -461,12 +474,15 @@
                 dma((owners,)),
             ],
             compiler_params=pltpu.CompilerParams(
-                collective_id=0, has_side_effects=True, vmem_limit_bytes=60 * 1024 * 1024
+                collective_id=0, has_side_effects=True, vmem_limit_bytes=40 * 1024 * 1024
             ),
             name="fracture",
         )(
-            u_start, toughness, crack_label,
-            obs_weight.reshape(Z * R, S), sensor_cell.reshape(1, S),
+            *[
+                pltpu.with_memory_space_constraint(x, pltpu.HBM)
+                for x in (u_start, toughness, crack_label, obs_weight.reshape(Z * R, S))
+            ],
+            sensor_cell.reshape(1, S),
         )
 
     return jax.shard_map(

time: 44.1 us -> 41 us (0.930)
  Pallas kernels: 38.8 us -> 37.2 us
  local copies, waits for them, and re-layouts: 4.42 us -> 2.92 us
    pallas_call x1, Pallas kernels: 38.8 us -> 37.2 us  [local(): pl.pallas_call(make_kernel(Z, R, C, S, sizes, owners), out_shape=(jax.Sha...]
    unnamed x5, local copies, waits for them, and re-layouts: 4.42 us -> 2.92 us
where the time goes in v2:
time: 41 us; the launch traced here: 40.8 us
  Pallas kernels  37.2 us (91%)
  local copies, waits for them, and re-layouts  2.92 us (7%)
  between operations  0.65 us (2%)
    pallas_call x1, Pallas kernels, local(): pl.pallas_call(make_kernel(Z, R, C, S, sizes, owners), out_shape=(jax.Sha...  37.2 us
    unnamed x5, local copies, waits for them, and re-layouts  2.92 us

profile of v2, /device:TPU:0, one launch (start us, length us, event | category | flops | bytes accessed | tf_op | source)
XLA Modules:
  0.0 40.8 jit_solution(17969032033260575380)
XLA Ops:
  0.6 0.0 copy-start
  0.6 0.7 %copy-done = s32[4096]{0:T(1024)S(1)} copy-done((s32[4096]{0:T(1024)S(1)}, s32[4096]{0:T(1024)}, u32[]{:S(2)}) %copy-start) | copy-done | bytes 16408
  1.4 37.2 %fracture.1 = (f32[3,8,32,256]{3,2,1,0:T(8,128)S(1)}, f32[8,32,256]{2,1,0:T(8,128)S(1)}, f32[3,4096]{1,0:T(4,128)S(1)}) custom-call(f32[3,8,32,256]{3,2,1,0:T(8,128)} %u_hbm.1, f32[8,32,256]{2,1,0:T(8,128)} %tough_hbm.1, s32[8,32,256]{2,1,0:T(8,128)} %crack_hbm.1, bf16[256,4096]{1,0:T(8,128)(2,1)} %bitcast.3, s32[1,4096]{1,0:T(1,128)S(1)} %bitcast.2), custom_call_target="tpu_custom_call" | custom-call | tf_op jit(solution)/shard_map/fracture/pallas_call | solution.py:444
  38.6 0.9 %copy.11 = f32[3,8,32,256]{3,2,1,0:T(8,128)} copy(f32[3,8,32,256]{3,2,1,0:T(8,128)S(1)} %get-tuple-element.6) | data formatting | bytes 1572864
  39.5 0.7 %copy.12 = f32[8,32,256]{2,1,0:T(8,128)} copy(f32[8,32,256]{2,1,0:T(8,128)S(1)} %get-tuple-element.7) | data formatting | bytes 524288
  40.2 0.6 %copy.13 = f32[3,4096]{1,0:T(4,128)} copy(f32[3,4096]{1,0:T(4,128)S(1)} %get-tuple-element.8) | data formatting | bytes 98304
Async XLA Ops:
  0.6 0.7 %copy-start = (s32[4096]{0:T(1024)S(1)}, s32[4096]{0:T(1024)}, u32[]{:S(2)}) copy-start(s32[4096]{0:T(1024)} %param.9) | copy-start | bytes 49156
